TPU v7x, 32 devices: a whole 2x2x4 slice. The times are simulated.
32 devices in a mesh: dp: 4 (over y, core), expert: 8 (over z, x).
Axes of the slice: x: 2, y: 2, z: 4, core: 2. Of those that a mesh axis runs over, the one named last changes fastest.
Arguments:
- hidden: bfloat16 [8192, 768], P(('dp', 'expert')), may hold values from -6 to 6
- w_down: bfloat16 [8, 768, 2048], P('expert', 'dp'), may hold values from -0.21875 to 0.21875
- expert_ids: int32 [1024, 4], P(('dp', 'expert')), may hold values from 0 to 7, all different within a row; in each aligned block of 32 rows (0 to 31, 32 to 63, ...) at most 32 rows name the same one
- gates: float32 [1024, 4], P(('dp', 'expert')), may hold values from 0.05 to 1
- cotangent: bfloat16 [1024, 2048], P(('dp', 'expert')), may hold values from -6 to 6
Outputs:
- mixed: bfloat16 [1024, 2048], P(('dp', 'expert'))
- gate_grads: float32 [1024, 4], P(('dp', 'expert'))
- hidden_grads: bfloat16 [8192, 768], P(('dp', 'expert'))
- weight_grads: bfloat16 [8, 768, 2048], P('expert', 'dp')
Inputs may be any that keep to these rules, and one draw needn't show every extreme that they name: `expert_ids`: each row names 4 different experts. Among the rows of one device no expert is named more than 32 times, a bound that some block reaches.
All inputs are finite; a program needn't handle non-finite values.
Results may differ from a plain program's by a relative error of at most 0.015.
Values may be sent and summed in bfloat16 or wider, within the bound.
A program may use at most 64 MiB of HBM per device.

v0:
```python
import jax
import jax.numpy as jnp
from jax import lax
from jax.sharding import PartitionSpec as P


def slot_table(expert_ids, experts, capacity):
    flat_ids = expert_ids.reshape(-1)
    choose = (flat_ids[:, None] == jnp.arange(experts, dtype=jnp.int32)[None, :]).astype(jnp.int32)
    earlier = jnp.cumsum(choose, axis=0) - choose
    position = jnp.sum(earlier * choose, axis=1)
    target = flat_ids * capacity + position
    return (target[None, :] == jnp.arange(experts * capacity, dtype=jnp.int32)[:, None]).astype(
        jnp.bfloat16
    )


def send_grads(placer, gates, cotangent, experts, capacity):
    width = cotangent.shape[1]
    scaled = gates[:, :, None] * cotangent.astype(jnp.float32)[:, None, :]
    routed = scaled.astype(jnp.bfloat16).reshape(-1, width)
    packed = jnp.dot(placer, routed, preferred_element_type=jnp.float32).astype(jnp.bfloat16)
    packed = packed.reshape(experts, capacity, width)
    arrived = lax.all_to_all(packed, "expert", split_axis=0, concat_axis=0, tiled=True)
    return arrived.reshape(experts * capacity, width)


def per_device(hidden, w_down, expert_ids, gates, cotangent):
    experts = lax.axis_size("expert")
    capacity = hidden.shape[0] // experts
    width = cotangent.shape[1]
    tok_count = expert_ids.shape[0]
    top_count = expert_ids.shape[1]
    weight_rows = w_down.reshape(w_down.shape[1], width)
    placer = slot_table(expert_ids, experts, capacity)
    full_weight = lax.all_gather(weight_rows, "dp", axis=0, tiled=True)
    outputs = jnp.dot(hidden, full_weight, preferred_element_type=jnp.float32)
    packed_out = outputs.astype(jnp.bfloat16).reshape(experts, capacity, width)
    returned = lax.all_to_all(packed_out, "expert", split_axis=0, concat_axis=0, tiled=True)
    picked = lax.dot_general(
        placer,
        returned.reshape(experts * capacity, width),
        (((0,), (0,)), ((), ())),
        preferred_element_type=jnp.float32,
    )
    picked = picked.reshape(tok_count, top_count, width)
    mixed = jnp.sum(gates[:, :, None] * picked, axis=1).astype(jnp.bfloat16)
    gate_grads = jnp.sum(picked * cotangent.astype(jnp.float32)[:, None, :], axis=2)
    grads_in = send_grads(placer, gates, cotangent, experts, capacity)
    hidden_grads = lax.dot_general(
        grads_in, full_weight, (((1,), (1,)), ((), ())), preferred_element_type=jnp.float32
    ).astype(jnp.bfloat16)
    partial_sum = lax.dot_general(
        hidden, grads_in, (((0,), (0,)), ((), ())), preferred_element_type=jnp.float32
    )
    rounded = lax.optimization_barrier(partial_sum.astype(jnp.bfloat16))
    weight_sums = lax.psum_scatter(
        rounded.astype(jnp.float32).astype(jnp.bfloat16), "dp", scatter_dimension=0, tiled=True
    )
    weight_grads = weight_sums.reshape(1, weight_rows.shape[0], width)
    return (mixed, gate_grads, hidden_grads, weight_grads)


def solution(mesh):
    placed = (
        P(("dp", "expert"), None),
        P("expert", "dp", None),
        P(("dp", "expert"), None),
        P(("dp", "expert"), None),
        P(("dp", "expert"), None),
    )
    return jax.shard_map(
        per_device,
        mesh=mesh,
        in_specs=placed,
        out_specs=(
            P(("dp", "expert"), None),
            P(("dp", "expert"), None),
            P(("dp", "expert"), None),
            P("expert", "dp", None),
        ),
        check_vma=False,
    )
```

profile of v0, /device:TPU:0, one launch (start us, length us, event | category | flops | bytes accessed | tf_op | source)
XLA Modules:
  0.0 96.7 jit_solution(4411713256529870389)
XLA Ops:
  7.2 0.7 all-gather.3.cloned.1.call-update
  8.0 0.8 copy.29
  8.7 0.1 reshape.62
  8.8 0.8 copy.31
  9.6 0.1 mul.59
  9.7 1.1 %mul.55.clone = f32[32,4,2048]{2,1,0:T(4,128)S(1)} broadcast(bf16[32,2048]{1,0:T(8,128)(2,1)} %param.9), dimensions={0,2} | broadcast | bytes 1179648 | tf_op jit(solution)/shard_map/mul | solution.py:48
  10.9 0.4 mul.61
  11.2 0.1 fusion.17
  11.3 0.2 reduce_window_sum.11
  11.5 0.2 select_reduce_fusion
  11.7 0.5 convolution_convert_fusion.1
  12.2 32.8 %all_to_all.10 = bf16[8,32,2048]{2,1,0:T(8,128)(2,1)S(1)} all-to-all(bf16[8,32,2048]{2,1,0:T(8,128)(2,1)S(1)} %bitcast.32), channel_id=1, replica_groups=mesh['dp'=4,'expert'=8] {'expert'}, dimensions={0} | all-to-all | bytes 2097152 | tf_op jit(solution)/shard_map/all_to_all | solution.py:24
  45.0 1.0 %copy-done.1 = bf16[8,32,2048]{2,1,0:T(8,128)(2,1)} copy-done((bf16[8,32,2048]{2,1,0:T(8,128)(2,1)}, bf16[8,32,2048]{2,1,0:T(8,128)(2,1)S(1)}, u32[]{:S(2)}) %copy-start.1) | copy-done | bytes 1048600
  46.0 1.0 %fusion.4 = bf16[768,2048]{0,1:T(8,128)(2,1)S(1)} fusion(bf16[256,2048]{1,0:T(8,128)(2,1)S(1)} %bitcast.29, bf16[256,768]{1,0:T(8,128)(2,1)S(1)} %copy-done), kind=kOutput, calls=%fused_computation.5 | convolution fusion | flops 806879232 | bytes 4587520 | tf_op jit(solution)/shard_map/dot_general | solution.py:53
  47.1 3.0 %copy.34 = bf16[768,2048]{1,0:T(8,128)(2,1)} copy(bf16[768,2048]{0,1:T(8,128)(2,1)S(1)} %fusion.4) | data formatting | bytes 6291456
  50.1 4.0 %fusion.5 = bf16[256,2048]{1,0:T(8,128)(2,1)} fusion(bf16[256,768]{1,0:T(8,128)(2,1)S(1)} %copy-done, bf16[1,768,2048]{2,1,0:T(8,128)(2,1)} %all-gather.3.cloned.1.call-done), kind=kOutput, calls=%fused_computation.7 | convolution fusion | flops 805830656 | bytes 4587520 | tf_op jit(solution)/shard_map/dot_general | solution.py:37
  54.1 3.6 %all-to-all-start = ((bf16[8,32,2048]{2,1,0:T(8,128)(2,1)}), bf16[8,32,2048]{2,1,0:T(8,128)(2,1)S(1)}, u32[]{:S(2)}, u32[]{:S(2)}) async-start(bf16[8,32,2048]{2,1,0:T(8,128)(2,1)} %bitcast.2), calls=%async_computation | async-start | bytes 2097152 | tf_op jit(solution)/shard_map/all_to_all | solution.py:39
  57.7 0.1 reduce_sum.30
  57.9 3.9 %fusion.8 = bf16[256,768]{1,0:T(8,128)(2,1)} fusion(bf16[256,2048]{1,0:T(8,128)(2,1)S(1)} %bitcast.30, bf16[1,768,2048]{2,1,0:T(8,128)(2,1)} %all-gather.3.cloned.1.call-done), kind=kOutput, calls=%fused_computation.8 | convolution fusion | flops 805502976 | bytes 4587520 | tf_op jit(solution)/shard_map/dot_general | solution.py:50
  61.8 21.4 %all-to-all-done = bf16[8,32,2048]{2,1,0:T(8,128)(2,1)S(1)} async-done(((bf16[8,32,2048]{2,1,0:T(8,128)(2,1)}), bf16[8,32,2048]{2,1,0:T(8,128)(2,1)S(1)}, u32[]{:S(2)}, u32[]{:S(2)}) %all-to-all-start) | async-done | bytes 1048608 | tf_op jit(solution)/shard_map/all_to_all | solution.py:39
  83.2 1.1 %multiply_reduce_fusion = (f32[32,4]{0,1:T(4,128)}, bf16[32,2048]{1,0:T(8,128)(2,1)}) fusion(f32[32,2048]{1,0:T(8,128)S(1)} %convert_element_type.35, f32[32,4]{0,1:T(4,128)S(1)} %copy-done.5, bf16[256,2048,1]{1,0,2:T(8,128)(2,1)S(1)} %bitcast.33, s32[32,4]{0,1:T(4,128)S(1)} %multiply_add_fusion), kind=kOutput, calls=%fused_computation.10 | convolution fusion | flops 135233408 | bytes 1443328 | tf_op jit(solution)/shard_map/dot_general | solution.py:40
  84.4 2.8 %reduce-scatter.4.cloned.1.call-done = bf16[192,2048]{1,0:T(8,128)(2,1)} async-done(((bf16[768,2048]{1,0:T(8,128)(2,1)}), bf16[192,2048]{1,0:T(8,128)(2,1)}) %reduce-scatter.4.cloned.1.call-update) | async-done | bytes 786448
  87.1 1.4 %copy.35 = bf16[192,2048]{0,1:T(8,128)(2,1)S(1)} copy(bf16[192,2048]{1,0:T(8,128)(2,1)} %reduce-scatter.4.cloned.1.call-done) | data formatting | bytes 1572864
  88.6 1.2 %copy.33 = bf16[1,192,2048]{2,1,0:T(8,128)(2,1)} copy(bf16[1,192,2048]{1,2,0:T(8,128)(2,1)S(1)} %bitcast.31) | data formatting | bytes 1572864
  (19 shorter events, 0.3 us)
Async XLA Ops:
  7.2 38.9 %copy-start = (bf16[256,768]{1,0:T(8,128)(2,1)S(1)}, bf16[256,768]{1,0:T(8,128)(2,1)}, u32[]{:S(2)}) copy-start(bf16[256,768]{1,0:T(8,128)(2,1)} %param.5) | copy-start | bytes 1179652
  7.2 42.9 %all-gather.3.cloned.1.call-start = ((), (), s32[]{:S(2)}) async-start(), calls=%async_computation.3 | async-start | bytes 3932160 | tf_op jit(solution)/shard_map/all_gather | solution.py:36
  7.9 79.2 %reduce-scatter.4.cloned.1.call-start = ((), (), s32[]{:S(2)}) async-start(), calls=%async_computation.4 | async-start | bytes 3932160
  45.0 1.0 %copy-start.1 = (bf16[8,32,2048]{2,1,0:T(8,128)(2,1)}, bf16[8,32,2048]{2,1,0:T(8,128)(2,1)S(1)}, u32[]{:S(2)}) copy-start(bf16[8,32,2048]{2,1,0:T(8,128)(2,1)S(1)} %all_to_all.10) | copy-start | bytes 3145732
  50.0 7.7 %copy-start.3 = (bf16[32,2048]{1,0:T(8,128)(2,1)S(1)}, bf16[32,2048]{1,0:T(8,128)(2,1)}, u32[]{:S(2)}) copy-start(bf16[32,2048]{1,0:T(8,128)(2,1)} %param.9) | copy-start | bytes 393220
  50.1 7.8 %copy-start.4 = (s32[32,4]{0,1:T(4,128)S(1)}, s32[32,4]{0,1:T(4,128)}, u32[]{:S(2)}) copy-start(s32[32,4]{0,1:T(4,128)} %param.7) | copy-start | bytes 1540
  50.1 7.8 %copy-start.2 = (bf16[8,32,2048]{2,1,0:T(8,128)(2,1)S(1)}, bf16[8,32,2048]{2,1,0:T(8,128)(2,1)}, u32[]{:S(2)}) copy-start(bf16[8,32,2048]{2,1,0:T(8,128)(2,1)} %copy-done.1) | copy-start | bytes 3145732
  54.1 29.2 %all-to-all-start = ((bf16[8,32,2048]{2,1,0:T(8,128)(2,1)}), bf16[8,32,2048]{2,1,0:T(8,128)(2,1)S(1)}, u32[]{:S(2)}, u32[]{:S(2)}) async-start(bf16[8,32,2048]{2,1,0:T(8,128)(2,1)} %bitcast.2), calls=%async_computation | async-start | bytes 2097152 | tf_op jit(solution)/shard_map/all_to_all | solution.py:39
  57.7 25.6 %copy-start.5 = (f32[32,4]{0,1:T(4,128)S(1)}, f32[32,4]{0,1:T(4,128)}, u32[]{:S(2)}) copy-start(f32[32,4]{0,1:T(4,128)} %param.8) | copy-start | bytes 1540
Sparse Core Ops, SparseCore 0:
  9.5 31.2 all-gather.2
  50.2 36.9 reduce-scatter.3
where the time goes:
time: 97 us; the launch traced here: 96.7 us
  blocking collectives  32.8 us (34%)
  waiting for transfers between devices  24.9 us (26%)
  between operations  14.2 us (15%)
  matrix products  10.5 us (11%)
  local copies, waits for them, and re-layouts  10.1 us (10%)
  starting transfers between devices  3.68 us (4%)
    all_to_all x1, blocking collectives, send_grads(): lax.all_to_all(packed, 'expert', split_axis=0, concat_axis=0, tiled=True)  32.8 us
    all_to_all x1, waiting for transfers between devices, per_device(): lax.all_to_all(packed_out, 'expert', split_axis=0, concat_axis=0, tiled=T...  21.4 us
    unnamed x17, local copies, waits for them, and re-layouts  8.18 us
    dot_general x1, matrix products, per_device(): outputs = jnp.dot(hidden, full_weight, preferred_element_type=jnp.float32)  3.95 us
    dot_general x1, matrix products, per_device(): lax.dot_general(grads_in, full_weight, (((1,), (1,)), ((), ())), preferre...  3.94 us
    all_to_all x1, starting transfers between devices, per_device(): lax.all_to_all(packed_out, 'expert', split_axis=0, concat_axis=0, tiled=T...  3.61 us
    unnamed x3, waiting for transfers between devices  3.48 us
  transfers between devices with their start and end apart: 3, of which 2 were waited for; matrix products, arithmetic and copies ran while one was open for 18% of the time, Pallas kernels for 0%

commit v1 on v0

v1 whole, which is shorter than its diff:
```python
import functools

import jax
import jax.numpy as jnp
from jax import lax
from jax.experimental import pallas as pl
from jax.experimental.pallas import tpu as pltpu
from jax.sharding import PartitionSpec as P

MESH = pl.DeviceIdType.MESH
F32 = jnp.float32
BF16 = jnp.bfloat16


def tile_of(size, want):
    while size % want:
        want //= 2
    return want


def kernel(
    nd, ne, chunks,
    hidden, w, ids, gates, cot,
    mixed, gate_grads, hidden_grads, weight_grads,
    wfull, cot_all, meta_send, meta_recv, gg_send, gg_recv,
    ht, gh, ght, z, wg_send1, wg_recv1, wg_send2, wg_recv2, wg_own,
    mx_send1, mx_recv1, mx_send2, mx_recv2, mx_own,
    wy_s, wy_r, wf_s, wf_r, cz_s, cz_r, cf_s, cf_r, me_s, me_r, gg_s, gg_r,
    g1_s, g1_r, g2_s, g2_r, m1_s, m1_r, m2_s, m2_r, loc,
):
    R, N = nd // 2, ne // 2
    rows, D = w.shape
    tok, topk = ids.shape
    F = hidden.shape[1]
    cap = hidden.shape[0] // ne
    T = ne * tok
    a, e = lax.axis_index("dp"), lax.axis_index("expert")
    r, c = a // 2, a % 2
    q, x = e // 2, e % 2
    tile = tile_of(D, 512)

    def to(a2, e2):
        return {"dp": a2, "expert": e2}

    def remote(src, dst, ss, rs, dev):
        return pltpu.make_async_remote_copy(
            src_ref=src, dst_ref=dst, send_sem=ss, recv_sem=rs, device_id=dev, device_id_type=MESH
        )

    barrier = pltpu.get_barrier_semaphore()
    for d in range(1, ne):
        pl.semaphore_signal(barrier, inc=1, device_id=to(a, (e + d) % ne), device_id_type=MESH)
    for d in range(1, R):
        pl.semaphore_signal(barrier, inc=1, device_id=to(((r + d) % R) * 2 + c, e), device_id_type=MESH)
    pl.semaphore_signal(barrier, inc=1, device_id=to(r * 2 + 1 - c, e), device_id_type=MESH)

    own_w = pltpu.make_async_copy(w, wfull.at[pl.ds(pl.multiple_of(a * rows, rows), rows)], loc.at[0])
    own_w.start()
    own_c = pltpu.make_async_copy(cot, cot_all.at[q, x], loc.at[1])
    own_c.start()

    eye = lax.broadcasted_iota(jnp.int32, (tok, tok), 0) == lax.broadcasted_iota(jnp.int32, (tok, tok), 1)
    upper = (
        lax.broadcasted_iota(jnp.int32, (tok, tok), 0) < lax.broadcasted_iota(jnp.int32, (tok, tok), 1)
    ).astype(F32)

    def to_row(col):
        return jnp.sum(jnp.where(eye, col, 0.0), axis=0, keepdims=True)

    def to_col(row):
        return jnp.sum(jnp.where(eye, row, 0.0), axis=1, keepdims=True)

    idf = ids[...].astype(F32)
    gat = gates[...]
    names = lax.broadcasted_iota(jnp.int32, (ne, tok), 0).astype(F32)
    id_rows = [to_row(idf[:, k : k + 1]) for k in range(topk)]
    choose = jnp.zeros((ne, tok), F32)
    gate_t = jnp.zeros((ne, tok), F32)
    for k in range(topk):
        hit = id_rows[k] == names
        choose = choose + jnp.where(hit, 1.0, 0.0)
        gate_t = gate_t + jnp.where(hit, to_row(gat[:, k : k + 1]), 0.0)
    position = jnp.dot(choose.astype(BF16), upper.astype(BF16), preferred_element_type=F32)
    slot_t = jnp.where(choose > 0.0, position, -1.0)
    meta_send[...] = jnp.zeros_like(meta_send)
    gg_send[...] = jnp.zeros_like(gg_send)
    for k in range(ne):
        meta_send[k // 2, k % 2, 0:1, 0:tok] = slot_t[k : k + 1, :]
        meta_send[k // 2, k % 2, 1:2, 0:tok] = gate_t[k : k + 1, :]
    meta_recv[q, x] = meta_send[q, x]

    pl.semaphore_wait(barrier, ne - 1 + R - 1 + 1)

    step = rows // chunks

    def w_rows(block, i):
        return pl.ds(pl.multiple_of(block * rows + i * step, step), step)

    wy, wf, cz, cf, me = {}, {}, {}, {}, {}
    order = sorted(range(1, N), key=lambda d: min(d, N - d))
    for d in range(1, ne):
        o = (e + d) % ne
        me[d] = remote(
            meta_send.at[o // 2, o % 2], meta_recv.at[q, x], me_s.at[d - 1], me_r.at[d - 1], to(a, o)
        )
        me[d].start()
    for i in range(chunks):
        for d in range(1, R):
            wy[d, i] = remote(
                w.at[pl.ds(i * step, step)], wfull.at[w_rows(a, i)],
                wy_s.at[(d - 1) * chunks + i], wy_r.at[(d - 1) * chunks + i],
                to(((r + d) % R) * 2 + c, e),
            )
            wy[d, i].start()
    for d in order:
        cz[d] = remote(
            cot, cot_all.at[q, x], cz_s.at[d - 1], cz_r.at[d - 1], to(a, ((q + d) % N) * 2 + x)
        )
        cz[d].start()
    cf[0] = remote(cot, cot_all.at[q, x], cf_s.at[0], cf_r.at[0], to(a, q * 2 + 1 - x))
    cf[0].start()
    for i in range(chunks):
        wf[0, i] = remote(
            w.at[pl.ds(i * step, step)], wfull.at[w_rows(a, i)],
            wf_s.at[i], wf_r.at[i], to(r * 2 + 1 - c, e),
        )
        wf[0, i].start()

    def forward_cot(d):
        src = (q - d + N) % N
        cz[d].wait_recv()
        cf[d] = remote(
            cot_all.at[src, x], cot_all.at[src, x], cf_s.at[d], cf_r.at[d], to(a, q * 2 + 1 - x)
        )
        cf[d].start()

    def forward_w(i):
        for d in range(1, R):
            block = ((r - d + R) % R) * 2 + c
            wy[d, i].wait_recv()
            wf[d, i] = remote(
                wfull.at[w_rows(block, i)], wfull.at[w_rows(block, i)],
                wf_s.at[d * chunks + i], wf_r.at[d * chunks + i], to(r * 2 + 1 - c, e),
            )
            wf[d, i].start()

    for d in range(1, ne):
        me[d].wait_recv()

    def route(b):
        return meta_recv[b // 2, b % 2, 0:1, 0:tok], meta_recv[b // 2, b % 2, 1:2, 0:tok]

    def placer(slot_row):
        return (lax.broadcasted_iota(jnp.int32, (cap, tok), 0).astype(F32) == slot_row).astype(BF16)

    for b in range(ne):
        slot_row, gate_row = route(b)
        rows_b = lax.dot_general(
            placer(slot_row), hidden[b * cap : (b + 1) * cap, :], (((0,), (0,)), ((), ())),
            preferred_element_type=F32,
        )
        ht[b // 2, b % 2] = rows_b.astype(BF16)
        gh[b // 2, b % 2] = (to_col(gate_row) * rows_b).astype(BF16)
    ght[...] = gh[...].reshape(T, F).astype(F32).T.astype(BF16)

    half = len(order) // 2
    for d in order[:half]:
        forward_cot(d)
    forward_w(0)
    for d in order[half:]:
        forward_cot(d)
    own_c.wait()
    for d in range(N):
        cf[d].wait_recv()

    def grad_block(block, store):
        left = ght[pl.ds(pl.multiple_of(block * rows, rows), rows), :]

        @pl.loop(0, D // tile)
        def _(j):
            cols = pl.ds(pl.multiple_of(j * tile, tile), tile)
            right = cot_all[:, :, :, cols].reshape(T, tile)
            store(cols, jnp.dot(left, right, preferred_element_type=F32))

    g1, g2, m1, m2, gg = {}, {}, {}, {}, {}
    for k in list(range(1, R)) + [0]:
        o = (r + k) % R

        def put1(cols, val, k=k):
            wg_send1[k, :, cols] = val.astype(BF16)

        grad_block(o * 2 + 1 - c, put1)
        g1[k] = remote(
            wg_send1.at[k], wg_recv1.at[k], g1_s.at[k], g1_r.at[k], to(r * 2 + 1 - c, e)
        )
        g1[k].start()
    mid = max(1, chunks // 2)
    for i in range(1, mid):
        forward_w(i)
    for k in range(1, R):
        o = (r + k) % R
        g1[k].wait_recv()

        def put2(cols, val, k=k):
            wg_send2[k - 1, :, cols] = (val + wg_recv1[k, :, cols].astype(F32)).astype(BF16)

        grad_block(o * 2 + c, put2)
        g2[k] = remote(
            wg_send2.at[k - 1], wg_recv2.at[k - 1], g2_s.at[k - 1], g2_r.at[k - 1], to(o * 2 + c, e)
        )
        g2[k].start()
    g1[0].wait_recv()

    def put3(cols, val):
        wg_own[:, cols] = val + wg_recv1[0, :, cols].astype(F32)

    grad_block(r * 2 + c, put3)

    for i in range(mid, chunks):
        forward_w(i)
    own_w.wait()
    for i in range(chunks):
        for d in range(R):
            wf[d, i].wait_recv()

    def out_block(column, store):
        left = gh[:, pl.ds(column, 1)].reshape(N * tok, F)

        @pl.loop(0, D // tile)
        def _(j):
            cols = pl.ds(pl.multiple_of(j * tile, tile), tile)
            val = jnp.dot(left, wfull[:, cols], preferred_element_type=F32)
            store(cols, val.reshape(N, tok, tile))

    def put4(cols, val):
        mx_send1[:, :, cols] = val.astype(BF16)

    out_block(1 - x, put4)
    for k in order + [0]:
        o = (q + k) % N
        m1[k] = remote(
            mx_send1.at[o], mx_recv1.at[o], m1_s.at[k], m1_r.at[k], to(a, q * 2 + 1 - x)
        )
        m1[k].start()

    def put5(cols, val):
        mx_own[:, :, cols] = val

    out_block(x, put5)

    ftile = tile_of(F, 256)
    @pl.loop(0, F // ftile)
    def _(j):
        part = pl.ds(pl.multiple_of(j * ftile, ftile), ftile)
        z[:, part] = lax.dot_general(
            cot_all[...].reshape(T, D), wfull[part, :], (((1,), (1,)), ((), ())),
            preferred_element_type=F32,
        )

    for k in order:
        o = (q + k) % N
        m1[k].wait_recv()
        mx_send2[o] = (mx_own[o] + mx_recv1[o].astype(F32)).astype(BF16)
        m2[k] = remote(
            mx_send2.at[o], mx_recv2.at[q], m2_s.at[k - 1], m2_r.at[k - 1], to(a, o * 2 + x)
        )
        m2[k].start()

    for b in range(ne):
        zb = z[b * tok : (b + 1) * tok, :]
        slot_row, gate_row = route(b)
        gg_col = jnp.sum(ht[b // 2, b % 2].astype(F32) * zb, axis=1, keepdims=True)
        gg_send[b // 2, b % 2, 0:1, 0:tok] = to_row(gg_col)
        scaled = (to_col(gate_row) * zb).astype(BF16)
        hidden_grads[b * cap : (b + 1) * cap, :] = jnp.dot(
            placer(slot_row), scaled, preferred_element_type=F32
        ).astype(BF16)
    for d in range(1, ne):
        o = (e + d) % ne
        gg[d] = remote(
            gg_send.at[o // 2, o % 2], gg_recv.at[q, x], gg_s.at[d - 1], gg_r.at[d - 1], to(a, o)
        )
        gg[d].start()
    gg_recv[q, x] = gg_send[q, x]

    m1[0].wait_recv()
    total = mx_own[q] + mx_recv1[q].astype(F32)
    for k in order:
        m2[k].wait_recv()
        total = total + mx_recv2[(q - k + N) % N].astype(F32)
    mixed[...] = total.astype(BF16)

    for d in range(1, ne):
        gg[d].wait_recv()
    lanes = lax.broadcasted_iota(jnp.int32, (tok, topk), 1)
    result = jnp.zeros((tok, topk), F32)
    for k in range(topk):
        row = jnp.zeros((1, tok), F32)
        for b in range(ne):
            row = row + jnp.where(id_rows[k] == float(b), gg_recv[b // 2, b % 2, 0:1, 0:tok], 0.0)
        result = jnp.where(lanes == k, to_col(row), result)
    gate_grads[...] = result

    for k in range(1, R):
        g2[k].wait_recv()

    @pl.loop(0, D // tile)
    def _(j):
        cols = pl.ds(pl.multiple_of(j * tile, tile), tile)
        val = wg_own[:, cols]
        for k in range(1, R):
            val = val + wg_recv2[k - 1, :, cols].astype(F32)
        weight_grads[:, cols] = val.astype(BF16)

    for group in (wy, wf, cz, cf, me, g1, g2, m1, m2, gg):
        for copy in group.values():
            copy.wait_send()


def fused(hidden, weight_rows, expert_ids, gates, cotangent):
    nd, ne = lax.axis_size("dp"), lax.axis_size("expert")
    rows, D = weight_rows.shape
    tok, topk = expert_ids.shape
    F = hidden.shape[1]
    T, R, N = ne * tok, nd // 2, ne // 2
    chunks = 4
    while rows % (chunks * 16):
        chunks //= 2
    vm = pltpu.VMEM
    sem = lambda n: pltpu.SemaphoreType.DMA((max(n, 1),))
    spec = pl.BlockSpec(memory_space=pltpu.VMEM)
    return pl.pallas_call(
        functools.partial(kernel, nd, ne, chunks),
        out_shape=(
            jax.ShapeDtypeStruct((tok, D), BF16),
            jax.ShapeDtypeStruct((tok, topk), F32),
            jax.ShapeDtypeStruct(hidden.shape, BF16),
            jax.ShapeDtypeStruct((rows, D), BF16),
        ),
        in_specs=[spec] * 5,
        out_specs=(spec,) * 4,
        scratch_shapes=[
            vm((F, D), BF16), vm((N, 2, tok, D), BF16),
            vm((N, 2, 8, 128), F32), vm((N, 2, 8, 128), F32),
            vm((N, 2, 8, 128), F32), vm((N, 2, 8, 128), F32),
            vm((N, 2, tok, F), BF16), vm((N, 2, tok, F), BF16), vm((F, T), BF16), vm((T, F), F32),
            vm((R, rows, D), BF16), vm((R, rows, D), BF16),
            vm((max(R - 1, 1), rows, D), BF16), vm((max(R - 1, 1), rows, D), BF16), vm((rows, D), F32),
            vm((N, tok, D), BF16), vm((N, tok, D), BF16),
            vm((N, tok, D), BF16), vm((N, tok, D), BF16), vm((N, tok, D), F32),
            sem((R - 1) * chunks), sem((R - 1) * chunks), sem(R * chunks), sem(R * chunks),
            sem(N - 1), sem(N - 1), sem(N), sem(N),
            sem(ne - 1), sem(ne - 1), sem(ne - 1), sem(ne - 1),
            sem(R), sem(R), sem(R - 1), sem(R - 1),
            sem(N), sem(N), sem(N - 1), sem(N - 1), sem(2),
        ],
        compiler_params=pltpu.CompilerParams(
            collective_id=0, has_side_effects=True, vmem_limit_bytes=60 * 1024 * 1024
        ),
    )(hidden, weight_rows, expert_ids, gates, cotangent)


def slot_table(expert_ids, experts, capacity):
    flat_ids = expert_ids.reshape(-1)
    choose = (flat_ids[:, None] == jnp.arange(experts, dtype=jnp.int32)[None, :]).astype(jnp.int32)
    earlier = jnp.cumsum(choose, axis=0) - choose
    position = jnp.sum(earlier * choose, axis=1)
    target = flat_ids * capacity + position
    return (target[None, :] == jnp.arange(experts * capacity, dtype=jnp.int32)[:, None]).astype(BF16)


def plain(hidden, weight_rows, expert_ids, gates, cotangent):
    experts = lax.axis_size("expert")
    capacity = hidden.shape[0] // experts
    tok, topk = expert_ids.shape
    width = cotangent.shape[1]
    table = slot_table(expert_ids, experts, capacity)
    weight = lax.all_gather(weight_rows, "dp", axis=0, tiled=True)
    outputs = jnp.dot(hidden, weight, preferred_element_type=F32).astype(BF16)
    back = lax.all_to_all(outputs, "expert", split_axis=0, concat_axis=0, tiled=True)
    picked = lax.dot_general(table, back, (((0,), (0,)), ((), ())), preferred_element_type=F32)
    picked = picked.reshape(tok, topk, width)
    cot32 = cotangent.astype(F32)[:, None, :]
    mixed = jnp.sum(gates[:, :, None] * picked, axis=1).astype(BF16)
    gate_grads = jnp.sum(picked * cot32, axis=2)
    routed = (gates[:, :, None] * cot32).astype(BF16).reshape(-1, width)
    packed = jnp.dot(table, routed, preferred_element_type=F32).astype(BF16)
    grads = lax.all_to_all(packed, "expert", split_axis=0, concat_axis=0, tiled=True)
    hidden_grads = lax.dot_general(
        grads, weight, (((1,), (1,)), ((), ())), preferred_element_type=F32
    ).astype(BF16)
    partial = lax.dot_general(
        hidden, grads, (((0,), (0,)), ((), ())), preferred_element_type=F32
    ).astype(BF16)
    sums = lax.psum_scatter(partial, "dp", scatter_dimension=0, tiled=True)
    return mixed, gate_grads, hidden_grads, sums


def per_device(hidden, w_down, expert_ids, gates, cotangent):
    nd, ne = lax.axis_size("dp"), lax.axis_size("expert")
    rows, width = w_down.shape[1:]
    cap, tok = hidden.shape[0] // ne, expert_ids.shape[0]
    tiled = rows % 16 == 0 and cap % 16 == 0 and tok % 16 == 0 and tok <= 128
    paired = nd % 2 == 0 and ne % 2 == 0
    body = fused if tiled and paired else plain
    mixed, gate_grads, hidden_grads, sums = body(
        hidden, w_down.reshape(rows, width), expert_ids, gates, cotangent
    )
    return mixed, gate_grads, hidden_grads, sums.reshape(1, rows, width)


def solution(mesh):
    split = P(("dp", "expert"), None)
    weights = P("expert", "dp", None)
    return jax.shard_map(
        per_device,
        mesh=mesh,
        in_specs=(split, weights, split, split, split),
        out_specs=(split, split, split, weights),
        check_vma=False,
    )
```

time: 97 us -> 60.9 us (0.63)
  Pallas kernels: 0 us -> 52.3 us
  blocking collectives: 32.8 us -> 0 us
  waiting for transfers between devices: 24.9 us -> 0 us
  between operations: 14.2 us -> 0.66 us
  matrix products: 10.5 us -> 0 us
  starting transfers between devices: 3.68 us -> 0 us
  local copies, waits for them, and re-layouts: 10.1 us -> 7.73 us
    pallas_call x0 -> x1, Pallas kernels: none -> 52.3 us  [fused(): pl.pallas_call(functools.partial(kernel, nd, ne, chunks), out_shape=(jax....]
    all_to_all x1 -> x0, blocking collectives: 32.8 us -> none  [send_grads(): lax.all_to_all(packed, 'expert', split_axis=0, concat_axis=0, tiled=True)]
    all_to_all x1 -> x0, waiting for transfers between devices: 21.4 us -> none  [per_device(): lax.all_to_all(packed_out, 'expert', split_axis=0, concat_axis=0, tiled=T...]
    dot_general x5 -> x0, matrix products: 10.5 us -> none  [the longest x1 3.95 us: per_device(): outputs = jnp.dot(hidden, full_weight, preferred_element_type=jnp.float32)]
    all_to_all x1 -> x0, starting transfers between devices: 3.61 us -> none  [per_device(): lax.all_to_all(packed_out, 'expert', split_axis=0, concat_axis=0, tiled=T...]
    unnamed x3 -> x0, waiting for transfers between devices: 3.48 us -> none
    mul x3 -> x0, local copies, waits for them, and re-layouts: 1.61 us -> none  [the longest x2 1.51 us: per_device(): picked * cotangent.astype(jnp.float32)[:, None, :]]
    unnamed x17 -> x10, local copies, waits for them, and re-layouts: 8.18 us -> 7.73 us
  transfers between devices with their start and end apart: 3 -> 0, of which waited for: 2 -> 0; matrix products, arithmetic and copies ran while one was open for 18% -> 0% of each run, Pallas kernels for 0% -> 0%
where the time goes in v1:
time: 60.9 us; the launch traced here: 60.7 us
  Pallas kernels  52.3 us (86%)
  local copies, waits for them, and re-layouts  7.73 us (13%)
  between operations  0.66 us (1%)
    pallas_call x1, Pallas kernels, fused(): pl.pallas_call(functools.partial(kernel, nd, ne, chunks), out_shape=(jax....  52.3 us
    unnamed x10, local copies, waits for them, and re-layouts  7.73 us

profile of v1, /device:TPU:0, one launch (start us, length us, event | category | flops | bytes accessed | tf_op | source)
XLA Modules:
  0.0 60.7 jit_solution(12838306201376840368)
XLA Ops:
  0.6 0.0 copy-start.1
  0.6 1.4 %copy.9.ids = s32[32,4]{1,0:T(8,128)} copy(s32[32,4]{0,1:T(4,128)} %param.7) | data formatting | bytes 1024 | tf_op args[2]
  2.0 0.0 copy-done.1
  2.0 0.7 %copy.10.gates = f32[32,4]{1,0:T(8,128)} copy(f32[32,4]{0,1:T(4,128)S(1)} %copy-done.1) | data formatting | bytes 1024 | tf_op args[3]
  2.7 52.3 %shard_map.84 = (bf16[32,2048]{1,0:T(8,128)(2,1)}, f32[32,4]{1,0:T(8,128)}, bf16[256,768]{1,0:T(8,128)(2,1)}, bf16[192,2048]{1,0:T(8,128)(2,1)}) custom-call(bf16[256,768]{1,0:T(8,128)(2,1)} %hidden.1, bf16[192,2048]{1,0:T(8,128)(2,1)} %bitcast.3, s32[32,4]{1,0:T(8,128)} %copy.9.ids, f32[32,4]{1,0:T(8,128)} %copy.10.gates, bf16[32,2048]{1,0:T(8,128)(2,1)} %cot.1), custom_call_target="tpu_custom_call" | custom-call | tf_op jit(solution)/shard_map/pallas_call | solution.py:332
  55.0 0.0 copy-start
  55.0 1.4 %copy.11 = f32[32,4]{0,1:T(4,128)} copy(f32[32,4]{1,0:T(8,128)} %get-tuple-element.13) | data formatting | bytes 1024
  56.5 1.6 %copy.15 = bf16[32,2048]{1,0:T(8,128)(2,1)} copy(bf16[32,2048]{1,0:T(8,128)(2,1)} %get-tuple-element.20) | data formatting | bytes 262144
  58.0 1.8 %copy.16 = bf16[256,768]{1,0:T(8,128)(2,1)} copy(bf16[256,768]{1,0:T(8,128)(2,1)} %get-tuple-element.22) | data formatting | bytes 786432
  59.8 0.0 copy-done
  59.8 0.9 %copy.17 = bf16[1,192,2048]{2,1,0:T(8,128)(2,1)} copy(bf16[1,192,2048]{2,1,0:T(8,128)(2,1)S(1)} %bitcast.2) | data formatting | bytes 1572864
Async XLA Ops:
  0.6 1.4 %copy-start.1 = (f32[32,4]{0,1:T(4,128)S(1)}, f32[32,4]{0,1:T(4,128)}, u32[]{:S(2)}) copy-start(f32[32,4]{0,1:T(4,128)} %param.8) | copy-start | bytes 1540
  55.0 4.8 %copy-start = (bf16[192,2048]{1,0:T(8,128)(2,1)S(1)}, bf16[192,2048]{1,0:T(8,128)(2,1)}, u32[]{:S(2)}) copy-start(bf16[192,2048]{1,0:T(8,128)(2,1)} %get-tuple-element.11) | copy-start | bytes 2359300

commit v2 on v1

v2 whole, which is shorter than its diff:
```python
import functools

import jax
import jax.numpy as jnp
from jax import lax
from jax.experimental import pallas as pl
from jax.experimental.pallas import tpu as pltpu
from jax.sharding import PartitionSpec as P

MESH = pl.DeviceIdType.MESH
F32 = jnp.float32
BF16 = jnp.bfloat16


VMEM_BYTES = 67043328


def kernel(
    nd, ne, C,
    hidden_in, w, ids, gates, cot,
    mixed, gate_grads, hidden_grads, weight_grads,
    hidden, wfull, cot_all, meta_send, meta_recv, gg_send, gg_recv,
    ht, gh, ght, z, wg_send1, wg_recv1, wg_send2, wg_recv2, wg_own,
    mx_send1, mx_recv1, mx_send2, mx_recv2, mx_own,
    wy_s, wy_r, wf_s, wf_r, cz_s, cz_r, cf_s, cf_r, me_s, me_r, gg_s, gg_r,
    g1_s, g1_r, g2_s, g2_r, m1_s, m1_r, m2_s, m2_r, lw, lc, lh,
):
    R, N = nd // 2, ne // 2
    rows, D = w.shape
    topk, tok = ids.shape
    F = hidden.shape[1]
    cap = hidden.shape[0] // ne
    T, cw = ne * tok, D // C
    a, e = lax.axis_index("dp"), lax.axis_index("expert")
    r, c = a // 2, a % 2
    q, x = e // 2, e % 2

    def to(a2, e2):
        return {"dp": a2, "expert": e2}

    def remote(src, dst, ss, rs, dev):
        copy = pltpu.make_async_remote_copy(
            src_ref=src, dst_ref=dst, send_sem=ss, recv_sem=rs, device_id=dev, device_id_type=MESH
        )
        copy.start()
        return copy

    def w_rows(block):
        return pl.ds(pl.multiple_of(block * rows, rows), rows)

    def cols(j):
        return slice(j * cw, (j + 1) * cw)

    barrier = pltpu.get_barrier_semaphore()
    for d in range(1, ne):
        pl.semaphore_signal(barrier, inc=1, device_id=to(a, (e + d) % ne), device_id_type=MESH)
    for d in range(1, R):
        pl.semaphore_signal(barrier, inc=1, device_id=to(((r + d) % R) * 2 + c, e), device_id_type=MESH)
    pl.semaphore_signal(barrier, inc=1, device_id=to(r * 2 + 1 - c, e), device_id_type=MESH)
    own_w, own_c = [], []
    for j in range(C):
        own_w.append(pltpu.make_async_copy(w.at[:, cols(j)], wfull.at[j, w_rows(a)], lw.at[j]))
        own_c.append(pltpu.make_async_copy(cot.at[:, cols(j)], cot_all.at[j, q, x], lc.at[j]))
        own_w[j].start()
        own_c[j].start()
    own_h = pltpu.make_async_copy(hidden_in, hidden, lh.at[0])
    own_h.start()

    eye = lax.broadcasted_iota(jnp.int32, (tok, tok), 0) == lax.broadcasted_iota(jnp.int32, (tok, tok), 1)
    upper = (
        lax.broadcasted_iota(jnp.int32, (tok, tok), 0) < lax.broadcasted_iota(jnp.int32, (tok, tok), 1)
    ).astype(F32)

    def to_row(col):
        return jnp.sum(jnp.where(eye, col, 0.0), axis=0, keepdims=True)

    def to_col(row):
        return jnp.sum(jnp.where(eye, row, 0.0), axis=1, keepdims=True)

    idf = ids[...].astype(F32)
    gat = gates[...]
    names = lax.broadcasted_iota(jnp.int32, (ne, tok), 0).astype(F32)
    id_rows = [idf[k : k + 1, :] for k in range(topk)]
    choose = jnp.zeros((ne, tok), F32)
    gate_t = jnp.zeros((ne, tok), F32)
    for k in range(topk):
        hit = id_rows[k] == names
        choose = choose + jnp.where(hit, 1.0, 0.0)
        gate_t = gate_t + jnp.where(hit, gat[k : k + 1, :], 0.0)
    position = jnp.dot(choose.astype(BF16), upper.astype(BF16), preferred_element_type=F32)
    slot_t = jnp.where(choose > 0.0, position, -1.0)
    meta_send[...] = jnp.zeros_like(meta_send)
    gg_send[...] = jnp.zeros_like(gg_send)
    for k in range(ne):
        meta_send[k // 2, k % 2, 0:1, 0:tok] = slot_t[k : k + 1, :]
        meta_send[k // 2, k % 2, 1:2, 0:tok] = gate_t[k : k + 1, :]
    meta_recv[q, x] = meta_send[q, x]

    pl.semaphore_wait(barrier, ne - 1 + R - 1 + 1)

    wy, wf, cz, cf, me, g1, g2, m1, m2, gg = ({} for _ in range(10))
    order = sorted(range(1, N), key=lambda d: min(d, N - d))
    pair_e, pair_d = to(a, q * 2 + 1 - x), to(r * 2 + 1 - c, e)
    for d in range(1, ne):
        o = (e + d) % ne
        me[d] = remote(
            meta_send.at[o // 2, o % 2], meta_recv.at[q, x], me_s.at[d - 1], me_r.at[d - 1], to(a, o)
        )
    for j in range(C):
        own_w[j].wait()
        own_c[j].wait()
        mine = wfull.at[j, w_rows(a)]
        for d in range(1, R):
            wy[d, j] = remote(
                mine, mine, wy_s.at[d - 1, j], wy_r.at[d - 1, j], to(((r + d) % R) * 2 + c, e)
            )
        ours = cot_all.at[j, q, x]
        for d in order:
            cz[d, j] = remote(
                ours, ours, cz_s.at[d - 1, j], cz_r.at[d - 1, j], to(a, ((q + d) % N) * 2 + x)
            )
        cf[0, j] = remote(ours, ours, cf_s.at[0, j], cf_r.at[0, j], pair_e)
        wf[0, j] = remote(mine, mine, wf_s.at[0, j], wf_r.at[0, j], pair_d)

    def forward_cot(j):
        for d in order:
            block = cot_all.at[j, (q - d + N) % N, x]
            cz[d, j].wait_recv()
            cf[d, j] = remote(block, block, cf_s.at[d, j], cf_r.at[d, j], pair_e)

    def forward_w(j):
        for d in range(1, R):
            block = wfull.at[j, w_rows(((r - d + R) % R) * 2 + c)]
            wy[d, j].wait_recv()
            wf[d, j] = remote(block, block, wf_s.at[d, j], wf_r.at[d, j], pair_d)

    own_h.wait()
    for d in range(1, ne):
        me[d].wait_recv()

    def route(b):
        return meta_recv[b // 2, b % 2, 0:1, 0:tok], meta_recv[b // 2, b % 2, 1:2, 0:tok]

    def placer(slot_row):
        return (lax.broadcasted_iota(jnp.int32, (cap, tok), 0).astype(F32) == slot_row).astype(BF16)

    for b in range(ne):
        slot_row, gate_row = route(b)
        rows_b = lax.dot_general(
            placer(slot_row), hidden[b * cap : (b + 1) * cap, :], (((0,), (0,)), ((), ())),
            preferred_element_type=F32,
        )
        ht[b // 2, b % 2] = rows_b.astype(BF16)
        gh[b // 2, b % 2] = (to_col(gate_row) * rows_b).astype(BF16)
    ght[...] = gh[...].reshape(T, F).astype(F32).T.astype(BF16)

    def cot_part(j):
        forward_cot(j)

    def grads_part(j):
        for d in range(N):
            cf[d, j].wait_recv()
        right = cot_all[j].reshape(T, cw)

        def block_of(block):
            return jnp.dot(ght[w_rows(block), :], right, preferred_element_type=F32)

        for k in range(R):
            wg_send1[j, k] = block_of(((r + k) % R) * 2 + 1 - c).astype(BF16)
        g1[j] = remote(wg_send1.at[j], wg_recv1.at[j], g1_s.at[j], g1_r.at[j], pair_d)
        for k in range(R):
            val = block_of(((r + k) % R) * 2 + c)
            if k == 0:
                wg_own[j] = val
            else:
                wg_hold = val
                if k == 1:
                    g1[j].wait_recv()
                wg_send2[j, k - 1] = (wg_hold + wg_recv1[j, k].astype(F32)).astype(BF16)
                g2[k, j] = remote(
                    wg_send2.at[j, k - 1], wg_recv2.at[j, k - 1], g2_s.at[k - 1, j], g2_r.at[k - 1, j],
                    to(((r + k) % R) * 2 + c, e),
                )
        if R == 1:
            g1[j].wait_recv()

    def out_part(j):
        forward_w(j)
        for d in range(R):
            wf[d, j].wait_recv()
        left = gh[:, pl.ds(1 - x, 1)].reshape(N * tok, F)
        val = jnp.dot(left, wfull[j], preferred_element_type=F32)
        mx_send1[j] = val.astype(BF16).reshape(N, tok, cw)
        m1[j] = remote(mx_send1.at[j], mx_recv1.at[j], m1_s.at[j], m1_r.at[j], pair_e)
        left = gh[:, pl.ds(x, 1)].reshape(N * tok, F)
        val = jnp.dot(left, wfull[j], preferred_element_type=F32)
        mx_own[j] = val.reshape(N, tok, cw)

    def z_part(j):
        val = lax.dot_general(
            cot_all[j].reshape(T, cw), wfull[j], (((1,), (1,)), ((), ())), preferred_element_type=F32
        )
        z[...] = val if j == 0 else z[...] + val

    def mix_part(j):
        m1[j].wait_recv()
        for k in order:
            o = (q + k) % N
            mx_send2[j, o] = (mx_own[j, o] + mx_recv1[j, o].astype(F32)).astype(BF16)
            m2[k, j] = remote(
                mx_send2.at[j, o], mx_recv2.at[j, q], m2_s.at[k - 1, j], m2_r.at[k - 1, j],
                to(a, o * 2 + x),
            )

    cot_part(0)
    for j in range(C):
        if j + 1 < C:
            cot_part(j + 1)
        out_part(j)
        grads_part(j)
        z_part(j)
        if j > 0:
            mix_part(j - 1)
    mix_part(C - 1)

    for b in range(ne):
        zb = z[b * tok : (b + 1) * tok, :]
        slot_row, gate_row = route(b)
        gg_col = jnp.sum(ht[b // 2, b % 2].astype(F32) * zb, axis=1, keepdims=True)
        gg_send[b // 2, b % 2, 0:1, 0:tok] = to_row(gg_col)
        scaled = (to_col(gate_row) * zb).astype(BF16)
        hidden_grads[b * cap : (b + 1) * cap, :] = jnp.dot(
            placer(slot_row), scaled, preferred_element_type=F32
        ).astype(BF16)
    for d in range(1, ne):
        o = (e + d) % ne
        gg[d] = remote(
            gg_send.at[o // 2, o % 2], gg_recv.at[q, x], gg_s.at[d - 1], gg_r.at[d - 1], to(a, o)
        )
    gg_recv[q, x] = gg_send[q, x]

    for j in range(C):
        total = mx_own[j, q] + mx_recv1[j, q].astype(F32)
        for k in order:
            m2[k, j].wait_recv()
            total = total + mx_recv2[j, (q - k + N) % N].astype(F32)
        mixed[:, cols(j)] = total.astype(BF16)

    for d in range(1, ne):
        gg[d].wait_recv()
    for k in range(topk):
        row = jnp.zeros((1, tok), F32)
        for b in range(ne):
            row = row + jnp.where(id_rows[k] == float(b), gg_recv[b // 2, b % 2, 0:1, 0:tok], 0.0)
        gate_grads[k : k + 1, :] = row

    for j in range(C):
        val = wg_own[j] + wg_recv1[j, 0].astype(F32)
        for k in range(1, R):
            g2[k, j].wait_recv()
            val = val + wg_recv2[j, k - 1].astype(F32)
        weight_grads[:, cols(j)] = val.astype(BF16)

    for group in (wy, wf, cz, cf, me, g1, g2, m1, m2, gg):
        for copy in group.values():
            copy.wait_send()


def store_kernel(count, *refs):
    sems = refs[-1]
    copies = [pltpu.make_async_copy(refs[i], refs[count + i], sems.at[i]) for i in range(count)]
    for copy in copies:
        copy.start()
    for copy in copies:
        copy.wait()


def fused(hidden, weight_rows, expert_ids, gates, cotangent):
    nd, ne = lax.axis_size("dp"), lax.axis_size("expert")
    rows, D = weight_rows.shape
    tok, topk = expert_ids.shape
    F = hidden.shape[1]
    T, R, N = ne * tok, nd // 2, ne // 2
    C = 4
    while D % (C * 128):
        C //= 2
    cw = D // C
    vm = pltpu.VMEM
    sem = lambda *n: pltpu.SemaphoreType.DMA(tuple(max(i, 1) for i in n))
    near, far = pl.BlockSpec(memory_space=pltpu.VMEM), pl.BlockSpec(memory_space=pltpu.HBM)
    shapes = [((tok, D), BF16), ((topk, tok), F32), (hidden.shape, BF16), ((rows, D), BF16)]
    last = max(R - 1, 1)
    result_bytes = 2 * (tok * D + hidden.size + rows * D) + 128 * 1024
    results = pl.pallas_call(
        functools.partial(kernel, nd, ne, C),
        out_shape=tuple(pltpu.VMEM(*s) for s in shapes),
        in_specs=[far, far, near, near, far],
        out_specs=(near,) * 4,
        scratch_shapes=[
            vm(hidden.shape, BF16), vm((C, F, cw), BF16), vm((C, N, 2, tok, cw), BF16),
            vm((N, 2, 8, 128), F32), vm((N, 2, 8, 128), F32),
            vm((N, 2, 8, 128), F32), vm((N, 2, 8, 128), F32),
            vm((N, 2, tok, F), BF16), vm((N, 2, tok, F), BF16), vm((F, T), BF16), vm((T, F), F32),
            vm((C, R, rows, cw), BF16), vm((C, R, rows, cw), BF16),
            vm((C, last, rows, cw), BF16), vm((C, last, rows, cw), BF16), vm((C, rows, cw), F32),
            vm((C, N, tok, cw), BF16), vm((C, N, tok, cw), BF16),
            vm((C, N, tok, cw), BF16), vm((C, N, tok, cw), BF16), vm((C, N, tok, cw), F32),
            sem(R - 1, C), sem(R - 1, C), sem(R, C), sem(R, C),
            sem(N - 1, C), sem(N - 1, C), sem(N, C), sem(N, C),
            sem(ne - 1), sem(ne - 1), sem(ne - 1), sem(ne - 1),
            sem(C), sem(C), sem(R - 1, C), sem(R - 1, C),
            sem(C), sem(C), sem(N - 1, C), sem(N - 1, C), sem(C), sem(C), sem(1),
        ],
        compiler_params=pltpu.CompilerParams(
            collective_id=0, has_side_effects=True, vmem_limit_bytes=VMEM_BYTES - result_bytes
        ),
    )(hidden, weight_rows, expert_ids.T, gates.T, cotangent)
    mixed, gate_grads, hidden_grads, sums = pl.pallas_call(
        functools.partial(store_kernel, len(shapes)),
        out_shape=tuple(jax.ShapeDtypeStruct(*s) for s in shapes),
        in_specs=[pl.BlockSpec(memory_space=pl.ANY)] * 4,
        out_specs=(far,) * 4,
        scratch_shapes=[sem(len(shapes))],
        compiler_params=pltpu.CompilerParams(vmem_limit_bytes=1024 * 1024),
    )(*results)
    return mixed, gate_grads.T, hidden_grads, sums


def slot_table(expert_ids, experts, capacity):
    flat_ids = expert_ids.reshape(-1)
    choose = (flat_ids[:, None] == jnp.arange(experts, dtype=jnp.int32)[None, :]).astype(jnp.int32)
    earlier = jnp.cumsum(choose, axis=0) - choose
    position = jnp.sum(earlier * choose, axis=1)
    target = flat_ids * capacity + position
    return (target[None, :] == jnp.arange(experts * capacity, dtype=jnp.int32)[:, None]).astype(BF16)


def plain(hidden, weight_rows, expert_ids, gates, cotangent):
    experts = lax.axis_size("expert")
    capacity = hidden.shape[0] // experts
    tok, topk = expert_ids.shape
    width = cotangent.shape[1]
    table = slot_table(expert_ids, experts, capacity)
    weight = lax.all_gather(weight_rows, "dp", axis=0, tiled=True)
    outputs = jnp.dot(hidden, weight, preferred_element_type=F32).astype(BF16)
    back = lax.all_to_all(outputs, "expert", split_axis=0, concat_axis=0, tiled=True)
    picked = lax.dot_general(table, back, (((0,), (0,)), ((), ())), preferred_element_type=F32)
    picked = picked.reshape(tok, topk, width)
    cot32 = cotangent.astype(F32)[:, None, :]
    mixed = jnp.sum(gates[:, :, None] * picked, axis=1).astype(BF16)
    gate_grads = jnp.sum(picked * cot32, axis=2)
    routed = (gates[:, :, None] * cot32).astype(BF16).reshape(-1, width)
    packed = jnp.dot(table, routed, preferred_element_type=F32).astype(BF16)
    grads = lax.all_to_all(packed, "expert", split_axis=0, concat_axis=0, tiled=True)
    hidden_grads = lax.dot_general(
        grads, weight, (((1,), (1,)), ((), ())), preferred_element_type=F32
    ).astype(BF16)
    partial = lax.dot_general(
        hidden, grads, (((0,), (0,)), ((), ())), preferred_element_type=F32
    ).astype(BF16)
    sums = lax.psum_scatter(partial, "dp", scatter_dimension=0, tiled=True)
    return mixed, gate_grads, hidden_grads, sums


def per_device(hidden, w_down, expert_ids, gates, cotangent):
    nd, ne = lax.axis_size("dp"), lax.axis_size("expert")
    rows, width = w_down.shape[1:]
    cap, tok = hidden.shape[0] // ne, expert_ids.shape[0]
    tiled = rows % 16 == 0 and cap % 16 == 0 and tok % 16 == 0 and tok <= 128
    paired = nd % 2 == 0 and ne % 2 == 0
    body = fused if tiled and paired else plain
    mixed, gate_grads, hidden_grads, sums = body(
        hidden, w_down.reshape(rows, width), expert_ids, gates, cotangent
    )
    return mixed, gate_grads, hidden_grads, sums.reshape(1, rows, width)


def solution(mesh):
    split = P(("dp", "expert"), None)
    weights = P("expert", "dp", None)
    return jax.shard_map(
        per_device,
        mesh=mesh,
        in_specs=(split, weights, split, split, split),
        out_specs=(split, split, split, weights),
        check_vma=False,
    )
```

time: 60.9 us -> 46.2 us (0.76)
  local copies, waits for them, and re-layouts: 7.73 us -> 0 us
  Pallas kernels: 52.3 us -> 45.4 us
    unnamed x10 -> x0, local copies, waits for them, and re-layouts: 7.73 us -> none
    pallas_call x1 -> x2, Pallas kernels: 52.3 us -> 45.4 us  [the longest x1 44.3 us: fused(): pl.pallas_call(functools.partial(kernel, nd, ne, C), out_shape=tuple((plt...]
where the time goes in v2:
time: 46.2 us; the launch traced here: 46 us
  Pallas kernels  45.4 us (98%)
  between operations  0.64 us (1%)
    pallas_call x1, Pallas kernels, fused(): pl.pallas_call(functools.partial(kernel, nd, ne, C), out_shape=tuple((plt...  44.3 us
    pallas_call x1, Pallas kernels, fused(): pl.pallas_call(functools.partial(store_kernel, len(shapes)), out_shape=tu...  1.09 us

profile of v2, /device:TPU:0, one launch (start us, length us, event | category | flops | bytes accessed | tf_op | source)
XLA Modules:
  0.0 46.0 jit_solution(8639212226722482709)
XLA Ops:
  0.6 44.3 %shard_map.84 = (bf16[32,2048]{1,0:T(8,128)(2,1)S(1)}, f32[4,32]{1,0:T(4,128)S(1)}, bf16[256,768]{1,0:T(8,128)(2,1)S(1)}, bf16[192,2048]{1,0:T(8,128)(2,1)S(1)}) custom-call(bf16[256,768]{1,0:T(8,128)(2,1)} %hidden_in.1, bf16[192,2048]{1,0:T(8,128)(2,1)} %bitcast.5, s32[4,32]{1,0:T(4,128)} %bitcast.6, f32[4,32]{1,0:T(4,128)} %bitcast.7, bf16[32,2048]{1,0:T(8,128)(2,1)} %cot.1), custom_call_target="tpu_custom_call" | custom-call | tf_op jit(solution)/shard_map/pallas_call | solution.py:294
  45.0 1.1 %shard_map.85 = (bf16[32,2048]{1,0:T(8,128)(2,1)}, f32[4,32]{1,0:T(4,128)}, bf16[256,768]{1,0:T(8,128)(2,1)}, bf16[192,2048]{1,0:T(8,128)(2,1)}) custom-call(bf16[32,2048]{1,0:T(8,128)(2,1)S(1)} %get-tuple-element.12.refs_0_, f32[4,32]{1,0:T(4,128)S(1)} %get-tuple-element.13.refs_1_, bf16[256,768]{1,0:T(8,128)(2,1)S(1)} %get-tuple-element.14.refs_2_, ...), custom_call_target="tpu_custom_call" | custom-call | tf_op jit(solution)/shard_map/pallas_call | solution.py:318

commit v3 on v2

--- a/solution.py
+++ b/solution.py
@@ -19,10 +19,10 @@
     nd, ne, C,
     hidden_in, w, ids, gates, cot,
     mixed, gate_grads, hidden_grads, weight_grads,
-    hidden, wfull, cot_all, meta_send, meta_recv, gg_send, gg_recv,
+    hidden, wfull, cot_all, meta, gg_send, gg_recv,
     ht, gh, ght, z, wg_send1, wg_recv1, wg_send2, wg_recv2, wg_own,
     mx_send1, mx_recv1, mx_send2, mx_recv2, mx_own,
-    wy_s, wy_r, wf_s, wf_r, cz_s, cz_r, cf_s, cf_r, me_s, me_r, gg_s, gg_r,
+    wy_s, wy_r, wf_s, wf_r, cz_s, cz_r, cf_s, cf_r, gg_s, gg_r,
     g1_s, g1_r, g2_s, g2_r, m1_s, m1_r, m2_s, m2_r, lw, lc, lh,
 ):
     R, N = nd // 2, ne // 2
@@ -52,8 +52,16 @@
         return slice(j * cw, (j + 1) * cw)
 
     barrier = pltpu.get_barrier_semaphore()
-    for d in range(1, ne):
-        pl.semaphore_signal(barrier, inc=1, device_id=to(a, (e + d) % ne), device_id_type=MESH)
+    pl.semaphore_signal(barrier, inc=1, device_id=to(a, q * 2 + 1 - x), device_id_type=MESH)
+
+    @pl.when(q > 0)
+    def _():
+        pl.semaphore_signal(barrier, inc=1, device_id=to(a, (q - 1) * 2 + x), device_id_type=MESH)
+
+    @pl.when(q < N - 1)
+    def _():
+        pl.semaphore_signal(barrier, inc=1, device_id=to(a, (q + 1) * 2 + x), device_id_type=MESH)
+
     for d in range(1, R):
         pl.semaphore_signal(barrier, inc=1, device_id=to(((r + d) % R) * 2 + c, e), device_id_type=MESH)
     pl.semaphore_signal(barrier, inc=1, device_id=to(r * 2 + 1 - c, e), device_id_type=MESH)
@@ -89,23 +97,73 @@
         gate_t = gate_t + jnp.where(hit, gat[k : k + 1, :], 0.0)
     position = jnp.dot(choose.astype(BF16), upper.astype(BF16), preferred_element_type=F32)
     slot_t = jnp.where(choose > 0.0, position, -1.0)
-    meta_send[...] = jnp.zeros_like(meta_send)
+    meta[q, x] = jnp.zeros((2 * ne, 128), F32)
     gg_send[...] = jnp.zeros_like(gg_send)
-    for k in range(ne):
-        meta_send[k // 2, k % 2, 0:1, 0:tok] = slot_t[k : k + 1, :]
-        meta_send[k // 2, k % 2, 1:2, 0:tok] = gate_t[k : k + 1, :]
-    meta_recv[q, x] = meta_send[q, x]
-
-    pl.semaphore_wait(barrier, ne - 1 + R - 1 + 1)
-
-    wy, wf, cz, cf, me, g1, g2, m1, m2, gg = ({} for _ in range(10))
+    meta[q, x, 0:ne, 0:tok] = slot_t
+    meta[q, x, ne : 2 * ne, 0:tok] = gate_t
+
+    pl.semaphore_wait(barrier, R + 1 + (q + N - 1) // N + (2 * N - 2 - q) // N)
+
+    wy, wf, g1, g2, m1, m2, gg = ({} for _ in range(7))
     order = sorted(range(1, N), key=lambda d: min(d, N - d))
     pair_e, pair_d = to(a, q * 2 + 1 - x), to(r * 2 + 1 - c, e)
-    for d in range(1, ne):
-        o = (e + d) % ne
-        me[d] = remote(
-            meta_send.at[o // 2, o % 2], meta_recv.at[q, x], me_s.at[d - 1], me_r.at[d - 1], to(a, o)
-        )
+
+    def piece(j, i, column):
+        return cot_all.at[j, i, column] if j < C else meta.at[i, column]
+
+    def hop(j, s, i, side):
+        way = 1 if side == 0 else -1
+        return pltpu.make_async_remote_copy(
+            src_ref=piece(j, i, x), dst_ref=piece(j, i, x), send_sem=cz_s.at[side, s - 1, j],
+            recv_sem=cz_r.at[side, s - 1, j], device_id=to(a, (q + way) * 2 + x), device_id_type=MESH,
+        )
+
+    def cross(j, i, column):
+        return pltpu.make_async_remote_copy(
+            src_ref=piece(j, i, column), dst_ref=piece(j, i, column), send_sem=cf_s.at[i, j],
+            recv_sem=cf_r.at[i, j], device_id=pair_e, device_id_type=MESH,
+        )
+
+    def each_hop(act):
+        for side in range(2):
+            ahead = q < N - 1 if side == 0 else q > 0
+            for s in range(1, N):
+                held = q >= s - 1 if side == 0 else q + s - 1 < N
+
+                @pl.when(jnp.logical_and(ahead, held))
+                def _(side=side, s=s):
+                    act(s, q - s + 1 if side == 0 else q + s - 1, side)
+
+    def begin(j):
+        @pl.when(q < N - 1)
+        def _():
+            hop(j, 1, q, 0).start()
+
+        @pl.when(q > 0)
+        def _():
+            hop(j, 1, q, 1).start()
+
+        cross(j, q, x).start()
+
+    def relay(s):
+        for j in [C] + list(range(C)):
+            for side in range(2):
+                there = q >= s if side == 0 else q + s < N
+                onward = q < N - 1 if side == 0 else q > 0
+                i = q - s if side == 0 else q + s
+
+                @pl.when(there)
+                def _(j=j, side=side, i=i, onward=onward):
+                    hop(j, s, i, side).wait_recv()
+                    if s < N - 1:
+
+                        @pl.when(onward)
+                        def _():
+                            hop(j, s + 1, i, side).start()
+
+                    cross(j, i, x).start()
+
+    begin(C)
     for j in range(C):
         own_w[j].wait()
         own_c[j].wait()
@@ -114,19 +172,8 @@
             wy[d, j] = remote(
                 mine, mine, wy_s.at[d - 1, j], wy_r.at[d - 1, j], to(((r + d) % R) * 2 + c, e)
             )
-        ours = cot_all.at[j, q, x]
-        for d in order:
-            cz[d, j] = remote(
-                ours, ours, cz_s.at[d - 1, j], cz_r.at[d - 1, j], to(a, ((q + d) % N) * 2 + x)
-            )
-        cf[0, j] = remote(ours, ours, cf_s.at[0, j], cf_r.at[0, j], pair_e)
+        begin(j)
         wf[0, j] = remote(mine, mine, wf_s.at[0, j], wf_r.at[0, j], pair_d)
-
-    def forward_cot(j):
-        for d in order:
-            block = cot_all.at[j, (q - d + N) % N, x]
-            cz[d, j].wait_recv()
-            cf[d, j] = remote(block, block, cf_s.at[d, j], cf_r.at[d, j], pair_e)
 
     def forward_w(j):
         for d in range(1, R):
@@ -135,11 +182,15 @@
             wf[d, j] = remote(block, block, wf_s.at[d, j], wf_r.at[d, j], pair_d)
 
     own_h.wait()
-    for d in range(1, ne):
-        me[d].wait_recv()
+    for s in range(1, N):
+        relay(s)
+    for i in range(N):
+        cross(C, i, 1 - x).wait_recv()
 
     def route(b):
-        return meta_recv[b // 2, b % 2, 0:1, 0:tok], meta_recv[b // 2, b % 2, 1:2, 0:tok]
+        slot_row = meta[b // 2, b % 2, pl.ds(e, 1), :]
+        gate_row = meta[b // 2, b % 2, pl.ds(ne + e, 1), :]
+        return slot_row[:, 0:tok], gate_row[:, 0:tok]
 
     def placer(slot_row):
         return (lax.broadcasted_iota(jnp.int32, (cap, tok), 0).astype(F32) == slot_row).astype(BF16)
@@ -154,12 +205,9 @@
         gh[b // 2, b % 2] = (to_col(gate_row) * rows_b).astype(BF16)
     ght[...] = gh[...].reshape(T, F).astype(F32).T.astype(BF16)
 
-    def cot_part(j):
-        forward_cot(j)
-
     def grads_part(j):
-        for d in range(N):
-            cf[d, j].wait_recv()
+        for i in range(N):
+            cross(j, i, 1 - x).wait_recv()
         right = cot_all[j].reshape(T, cw)
 
         def block_of(block):
@@ -212,10 +260,7 @@
                 to(a, o * 2 + x),
             )
 
-    cot_part(0)
     for j in range(C):
-        if j + 1 < C:
-            cot_part(j + 1)
         out_part(j)
         grads_part(j)
         z_part(j)
@@ -261,9 +306,13 @@
             val = val + wg_recv2[j, k - 1].astype(F32)
         weight_grads[:, cols(j)] = val.astype(BF16)
 
-    for group in (wy, wf, cz, cf, me, g1, g2, m1, m2, gg):
+    for group in (wy, wf, g1, g2, m1, m2, gg):
         for copy in group.values():
             copy.wait_send()
+    for j in range(C + 1):
+        each_hop(lambda s, i, side, j=j: hop(j, s, i, side).wait_send())
+        for i in range(N):
+            cross(j, i, x).wait_send()
 
 
 def store_kernel(count, *refs):
@@ -298,16 +347,15 @@
         out_specs=(near,) * 4,
         scratch_shapes=[
             vm(hidden.shape, BF16), vm((C, F, cw), BF16), vm((C, N, 2, tok, cw), BF16),
-            vm((N, 2, 8, 128), F32), vm((N, 2, 8, 128), F32),
-            vm((N, 2, 8, 128), F32), vm((N, 2, 8, 128), F32),
+            vm((N, 2, 2 * ne, 128), F32), vm((N, 2, 8, 128), F32), vm((N, 2, 8, 128), F32),
             vm((N, 2, tok, F), BF16), vm((N, 2, tok, F), BF16), vm((F, T), BF16), vm((T, F), F32),
             vm((C, R, rows, cw), BF16), vm((C, R, rows, cw), BF16),
             vm((C, last, rows, cw), BF16), vm((C, last, rows, cw), BF16), vm((C, rows, cw), F32),
             vm((C, N, tok, cw), BF16), vm((C, N, tok, cw), BF16),
             vm((C, N, tok, cw), BF16), vm((C, N, tok, cw), BF16), vm((C, N, tok, cw), F32),
             sem(R - 1, C), sem(R - 1, C), sem(R, C), sem(R, C),
-            sem(N - 1, C), sem(N - 1, C), sem(N, C), sem(N, C),
-            sem(ne - 1), sem(ne - 1), sem(ne - 1), sem(ne - 1),
+            sem(2, N - 1, C + 1), sem(2, N - 1, C + 1), sem(N, C + 1), sem(N, C + 1),
+            sem(ne - 1), sem(ne - 1),
             sem(C), sem(C), sem(R - 1, C), sem(R - 1, C),
             sem(C), sem(C), sem(N - 1, C), sem(N - 1, C), sem(C), sem(C), sem(1),
         ],

time: 46.2 us -> 46.3 us (level)
  no operation moved by 1% of the time
where the time goes in v3:
time: 46.3 us; the launch traced here: 46.2 us
  Pallas kernels  45.5 us (98%)
  between operations  0.64 us (1%)
    pallas_call x1, Pallas kernels, fused(): pl.pallas_call(functools.partial(kernel, nd, ne, C), out_shape=tuple((plt...  44.4 us
    pallas_call x1, Pallas kernels, fused(): pl.pallas_call(functools.partial(store_kernel, len(shapes)), out_shape=tu...  1.09 us

profile of v3, /device:TPU:0, one launch (start us, length us, event | category | flops | bytes accessed | tf_op | source)
XLA Modules:
  0.0 46.2 jit_solution(6951179504959835724)
XLA Ops:
  0.6 44.4 %shard_map.84 = (bf16[32,2048]{1,0:T(8,128)(2,1)S(1)}, f32[4,32]{1,0:T(4,128)S(1)}, bf16[256,768]{1,0:T(8,128)(2,1)S(1)}, bf16[192,2048]{1,0:T(8,128)(2,1)S(1)}) custom-call(bf16[256,768]{1,0:T(8,128)(2,1)} %hidden_in.1, bf16[192,2048]{1,0:T(8,128)(2,1)} %bitcast.5, s32[4,32]{1,0:T(4,128)} %bitcast.6, f32[4,32]{1,0:T(4,128)} %bitcast.7, bf16[32,2048]{1,0:T(8,128)(2,1)} %cot.1), custom_call_target="tpu_custom_call" | custom-call | tf_op jit(solution)/shard_map/pallas_call | solution.py:343
  45.1 1.1 %shard_map.85 = (bf16[32,2048]{1,0:T(8,128)(2,1)}, f32[4,32]{1,0:T(4,128)}, bf16[256,768]{1,0:T(8,128)(2,1)}, bf16[192,2048]{1,0:T(8,128)(2,1)}) custom-call(bf16[32,2048]{1,0:T(8,128)(2,1)S(1)} %get-tuple-element.12.refs_0_, f32[4,32]{1,0:T(4,128)S(1)} %get-tuple-element.13.refs_1_, bf16[256,768]{1,0:T(8,128)(2,1)S(1)} %get-tuple-element.14.refs_2_, ...), custom_call_target="tpu_custom_call" | custom-call | tf_op jit(solution)/shard_map/pallas_call | solution.py:366
